TPU v7x, 32 devices: a whole 2x2x4 slice. The times are simulated.
32 devices in a mesh: groups: 2 (over x), seq: 4 (over y, core), head: 4 (over z).
Axes of the slice: x: 2, y: 2, z: 4, core: 2. Of those that a mesh axis runs over, the one named last changes fastest.
Arguments:
- query: bfloat16 [32, 16, 1024], P('groups', None, 'head'), parts along dimension 0, may hold values from -6 to 6, as said below
- new_key: bfloat16 [32, 16, 1024], P('groups', None, 'head'), parts along dimension 0, may hold values from -6 to 6
- new_value: bfloat16 [32, 16, 1024], P('groups', None, 'head'), parts along dimension 0, may hold values from -6 to 6
- keys: bfloat16 [32, 4096, 1024], P('groups', 'seq', 'head'), parts along dimension 0, may hold values from -6 to 6, as said below
- values: bfloat16 [32, 4096, 1024], P('groups', 'seq', 'head'), parts along dimension 0, may hold values from -6 to 6
- lengths: int32 [32], P('groups'), parts along dimension 0, may hold values from 2 to 4096
- time_bucket: int32 [32, 4096], P('groups', 'seq'), parts along dimension 0, may hold values from 0 to 63
- action: int32 [32, 4096], P('groups', 'seq'), parts along dimension 0, may hold values from 0 to 15
- time_bias: float32 [64, 8], P(None, 'head'), may hold values from -0.25 to 0.25
- action_bias: float32 [16, 8], P(None, 'head'), may hold values from -0.25 to 0.25
- gate: bfloat16 [32, 16, 1024], P('groups', None, 'head'), parts along dimension 0, may hold values from -6 to 6
- norm_gain: float32 [1024], P('head'), may hold values from 0.1 to 1.9
- w_out: bfloat16 [1024, 1024], P('head'), may hold values from -0.1875 to 0.1875
Outputs:
- output: bfloat16 [32, 16, 1024], P(('groups', 'seq'), None, 'head'), parts along dimension 0
There are 2 independent parts, one for each index of `groups`. A program takes and returns all parts, laid end to end along the dimension named above; an argument that names none is the same for every part. Nothing has to cross between parts.
Inputs may be any that keep to these rules, and one draw needn't show every extreme that they name: `query`: queries of order one; some users' queries may be large and equal to some of their keys. `keys`: keys of order one.
All inputs are finite; a program needn't handle non-finite values.
Results may differ from a plain program's by a relative error of at most 0.0056.
Values sent between devices are 32-bit elements; how exact they have to be, the bound alone decides.
No kernel may reach another device: no remote copies, remote signals or barrier semaphores. Data moves between devices by JAX's collectives and lax.ppermute only.
A program may use at most 64 MiB of HBM per device.

v0:
```python
import math

import jax
import jax.numpy as jnp
from jax import lax
from jax.sharding import PartitionSpec as P


def body(
    query,
    new_key,
    new_value,
    keys,
    values,
    lengths,
    time_bucket,
    action,
    time_bias,
    action_bias,
    gate,
    norm_gain,
    w_out,
):
    user_count, block_len, row_width = keys.shape
    cand_count = query.shape[1]
    head_count = time_bias.shape[1]
    head_size = row_width // head_count
    score_scale = 1.0 / math.sqrt(head_size)
    seq_count = lax.axis_size("seq")
    seq_rank = lax.axis_index("seq")
    query_heads = query.reshape(user_count, cand_count, head_count, head_size)
    key_heads = keys.reshape(user_count, block_len, head_count, head_size)
    value_heads = values.reshape(user_count, block_len, head_count, head_size)
    scores = (
        jnp.einsum("uchd,ushd->uchs", query_heads, key_heads, preferred_element_type=jnp.float32)
        * score_scale
    )
    bucket_onehot = (
        time_bucket[:, :, None] == jnp.arange(time_bias.shape[0], dtype=jnp.int32)[None, None, :]
    ).astype(jnp.float32)
    action_onehot = (
        action[:, :, None] == jnp.arange(action_bias.shape[0], dtype=jnp.int32)[None, None, :]
    ).astype(jnp.float32)
    biases = jnp.einsum("usb,bh->uhs", bucket_onehot, time_bias, precision=lax.Precision.HIGHEST)
    biases = biases + jnp.einsum(
        "usb,bh->uhs", action_onehot, action_bias, precision=lax.Precision.HIGHEST
    )
    scores = scores + biases[:, None]
    position = seq_rank * block_len + jnp.arange(block_len, dtype=jnp.int32)
    valid = position[None, None, None, :] < lengths[:, None, None, None]
    block_max = jnp.max(jnp.where(valid, scores, -1e30), axis=-1)
    weights = jnp.where(valid, jnp.exp(scores - block_max[..., None]), 0.0)
    block_sum = jnp.sum(weights, axis=-1)
    block_acc = jnp.einsum(
        "uchs,ushd->uchd",
        weights.astype(jnp.bfloat16),
        value_heads,
        preferred_element_type=jnp.float32,
    )
    local_users = user_count // seq_count
    first_user = seq_rank * local_users

    def own_rows(source):
        return lax.dynamic_slice_in_dim(source, first_user, local_users, 0)

    received = (
        lax.all_to_all(block_max[None], "seq", split_axis=1, concat_axis=0, tiled=True),
        lax.all_to_all(block_sum[None], "seq", split_axis=1, concat_axis=0, tiled=True),
        lax.all_to_all(block_acc[None], "seq", split_axis=1, concat_axis=0, tiled=True),
    )
    running_max = jnp.max(received[0], axis=0)
    factors = jnp.exp(received[0] - running_max[None])
    total = jnp.sum(factors * received[1], axis=0)
    accum = jnp.sum(factors[..., None] * received[2], axis=0)
    own_query = (
        own_rows(query).astype(jnp.float32).reshape(local_users, cand_count, head_count, head_size)
    )
    own_key = (
        own_rows(new_key)
        .astype(jnp.float32)
        .reshape(local_users, cand_count, head_count, head_size)
    )
    own_value = (
        own_rows(new_value)
        .astype(jnp.float32)
        .reshape(local_users, cand_count, head_count, head_size)
    )
    own_score = jnp.sum(own_query * own_key, axis=-1) * score_scale
    overall = jnp.maximum(running_max, own_score)
    past_factor = jnp.exp(running_max - overall)
    own_factor = jnp.exp(own_score - overall)
    attended = (past_factor[..., None] * accum + own_factor[..., None] * own_value) / (
        past_factor * total + own_factor
    )[..., None]
    local_squares = jnp.sum(jnp.square(attended), axis=(2, 3))
    full_width = row_width * lax.axis_size("head")
    gate_heads = (
        own_rows(gate).astype(jnp.float32).reshape(local_users, cand_count, head_count, head_size)
    )
    hidden = (attended * norm_gain.reshape(head_count, head_size) * jax.nn.silu(gate_heads)).astype(
        jnp.bfloat16
    )
    hidden = hidden.reshape(local_users * cand_count, row_width)
    partial_out = jnp.dot(hidden, w_out, preferred_element_type=jnp.float32).reshape(
        local_users, cand_count, -1
    )
    squares = lax.psum(local_squares, "head")
    projected = lax.psum_scatter(partial_out, "head", scatter_dimension=2, tiled=True)
    factor = 1.0 / jnp.sqrt(squares / full_width + 1e-06)
    return (projected * factor[:, :, None]).astype(jnp.bfloat16)


def solution(mesh):
    placed = (
        P("groups", None, "head"),
        P("groups", None, "head"),
        P("groups", None, "head"),
        P("groups", "seq", "head"),
        P("groups", "seq", "head"),
        P("groups"),
        P("groups", "seq"),
        P("groups", "seq"),
        P(None, "head"),
        P(None, "head"),
        P("groups", None, "head"),
        P("head"),
        P("head", None),
    )
    return jax.shard_map(
        body,
        mesh=mesh,
        in_specs=placed,
        out_specs=P(("groups", "seq"), None, "head"),
        check_vma=False,
    )
```

profile of v0, /device:TPU:0, one launch (start us, length us, event | category | flops | bytes accessed | tf_op | source)
XLA Modules:
  0.0 77.0 jit_solution(13217166976046112141)
XLA Ops:
  6.5 0.8 %broadcast_compare_fusion = pred[16,1024]{1,0:T(8,128)(4,1)S(1)} fusion(s32[1024]{0:T(1024)S(1)} %iota_add_fusion, s32[16]{0:T(128)} %param.18), kind=kLoop, calls=%fused_computation.49 | loop fusion | flops 16384 | bytes 20544 | tf_op jit(solution)/shard_map/lt | solution.py:50
  7.3 1.3 %fusion.24 = f32[16,1024,2]{1,2,0:T(2,128)S(1)} fusion(s32[16,1024]{1,0:T(8,128)} %param.20, f32[16,2]{0,1:T(2,128)} %param.22), kind=kOutput, calls=%fused_computation.26 | convolution fusion | flops 6553600 | bytes 196736 | tf_op jit(solution)/shard_map/usb,bh->uhs/dot_general | solution.py:45
  8.6 2.2 %fusion.17 = f32[16,2,1024]{2,1,0:T(2,128)S(1)} fusion(f32[16,1024,2]{1,2,0:T(2,128)S(1)} %fusion.24, s32[16,1024]{1,0:T(8,128)} %param.19, f32[64,2]{0,1:T(2,128)} %param.21), kind=kOutput, calls=%fused_computation.19 | convolution fusion | flops 26247168 | bytes 328192 | tf_op jit(solution)/shard_map/usb,bh->uhs/dot_general | solution.py:44
  10.8 5.8 %fusion.7 = (f32[16,16,2]{1,2,0:T(2,128)S(1)}, f32[16,2,1024,16]{2,3,1,0:T(8,128)S(1)}) fusion(f32[16,2,1024]{2,1,0:T(2,128)S(1)} %fusion.17, pred[16,1024]{1,0:T(8,128)(4,1)S(1)} %broadcast_compare_fusion, bf16[16,1024,256]{2,1,0:T(8,128)(2,1)} %param.16, bf16[16,16,256]{2,1,0:T(8,128)(2,1)} %param.13), kind=kOutput, calls=%fused_computation.10 | convolution fusion | flops 136314368 | bytes 10766336 | tf_op jit(solution)/shard_map/uchd,ushd->uchs/dot_general | solution.py:35
  16.6 0.7 reshape.128
  17.3 4.3 %all-to-all-start = ((f32[4,1,128]{2,1,0:T(1,128)}), f32[4,1,128]{2,1,0:T(1,128)S(1)}, u32[]{:S(2)}, u32[]{:S(2)}) async-start(f32[4,1,128]{2,1,0:T(1,128)} %reshape.128), calls=%async_computation | async-start | bytes 4096 | tf_op jit(solution)/shard_map/all_to_all | solution.py:67
  21.5 0.7 fusion.11
  22.3 5.6 %fusion.13 = f32[1,16,16,2,128]{4,2,3,0,1:T(8,128)} fusion(f32[16,2,1024,16]{2,3,1,0:T(8,128)S(1)} %get-tuple-element.13, f32[16,16,2]{1,2,0:T(2,128)S(1)} %get-tuple-element.12, f32[16,2,1024]{2,1,0:T(2,128)S(1)} %fusion.17, pred[16,1024]{1,0:T(8,128)(4,1)S(1)} %broadcast_compare_fusion, bf16[16,1024,256]{2,1,0:T(8,128)(2,1)} %param.17), kind=kOutput, calls=%fused_computation.17 | convolution fusion | flops 136839168 | bytes 10897408 | tf_op jit(solution)/shard_map/uchs,ushd->uchd/dot_general | solution.py:54
  27.9 0.7 reshape.130
  28.6 3.3 %all-to-all-start.2 = ((f32[4,1,128]{2,1,0:T(1,128)}), f32[4,1,128]{2,1,0:T(1,128)S(1)}, u32[]{:S(2)}, u32[]{:S(2)}) async-start(f32[4,1,128]{2,1,0:T(1,128)} %reshape.130), calls=%async_computation.2 | async-start | bytes 4096 | tf_op jit(solution)/shard_map/all_to_all | solution.py:68
  31.8 0.8 %convert_multiply_fusion.1 = f32[4,16,256]{2,1,0:T(8,128)S(1)} fusion(bf16[16,16,256]{2,1,0:T(8,128)(2,1)} %param.14, s32[]{:T(128)S(6)} %select_n.14, bf16[16,16,256]{2,1,0:T(8,128)(2,1)} %param.13), kind=kLoop, calls=%fused_computation.44 | loop fusion | flops 49152 | bytes 131076 | tf_op jit(solution)/shard_map/mul | solution.py:88
  32.7 0.1 reduce_sum.45
  32.8 0.1 copy.41
  32.9 0.6 broadcast.73
  33.5 0.6 reduce.2
  34.1 0.1 reshape.129
  34.2 1.3 %all-to-all-done.2 = f32[4,1,128]{2,1,0:T(1,128)S(1)} async-done(((f32[4,1,128]{2,1,0:T(1,128)}), f32[4,1,128]{2,1,0:T(1,128)S(1)}, u32[]{:S(2)}, u32[]{:S(2)}) %all-to-all-start.2) | async-done | bytes 2080 | tf_op jit(solution)/shard_map/all_to_all | solution.py:68
  35.6 3.4 %all-to-all-start.1 = ((f32[1,16,16,2,128]{4,2,3,0,1:T(8,128)}), f32[1,16,16,2,128]{4,2,3,0,1:T(8,128)S(1)}, u32[]{:S(2)}, u32[]{:S(2)}) async-start(f32[1,16,16,2,128]{4,2,3,0,1:T(8,128)} %fusion.13), calls=%async_computation.1 | async-start | bytes 524288 | tf_op jit(solution)/shard_map/all_to_all | solution.py:69
  39.0 0.6 reduce.1
  39.7 0.1 reshape.131
  39.8 0.1 copy.50
  39.9 0.1 div.27
  40.1 0.1 copy.48
  40.2 0.1 mul.128
  40.4 0.1 mul.129
  40.4 4.5 %all-to-all-done.1 = f32[1,16,16,2,128]{4,2,3,0,1:T(8,128)S(1)} async-done(((f32[1,16,16,2,128]{4,2,3,0,1:T(8,128)}), f32[1,16,16,2,128]{4,2,3,0,1:T(8,128)S(1)}, u32[]{:S(2)}, u32[]{:S(2)}) %all-to-all-start.1) | async-done | bytes 262176 | tf_op jit(solution)/shard_map/all_to_all | solution.py:69
  44.9 0.1 multiply_reduce_fusion
  45.1 0.9 %multiply_reduce_fusion.1 = (f32[4,16]{1,0:T(4,128)S(1)}, f32[4,16,256]{2,1,0:T(8,128)S(1)}) fusion(f32[4,16,256]{2,1,0:T(8,128)S(1)} %div.28, f32[4,16,256]{2,1,0:T(8,128)S(1)} %mul.129, bf16[16,16,256]{2,1,0:T(8,128)(2,1)} %param.15, s32[]{:T(128)S(6)} %select_n.14, f32[4,16,2,128]{3,1,2,0:T(8,128)S(1)} %multiply_reduce_fusion, f32[4,16,2]{1,2,0:T(2,128)S(1)} %copy.44), kind=kLoop, calls=%fused_computation.42 | loop fusion | flops 114624 | bytes 295684 | tf_op jit(solution)/shard_map/reduce_sum | solution.py:95
  46.0 1.7 %fusion.25 = f32[4,16,1024]{2,1,0:T(8,128)} fusion(bf16[256,1024]{1,0:T(8,128)(2,1)S(1)} %copy-done, f32[4,16,256]{2,1,0:T(8,128)S(1)} %get-tuple-element.6, bf16[16,16,256]{2,1,0:T(8,128)(2,1)} %param.23, s32[]{:T(128)S(6)} %select_n.14, f32[256]{0:T(256)S(1)} %copy-done.1), kind=kOutput, calls=%fused_computation.27 | convolution fusion | flops 33685504 | bytes 885764 | tf_op jit(solution)/shard_map/dot_general | solution.py:104
  47.7 12.4 %psum.7 = f32[4,16]{1,0:T(4,128)S(1)} all-reduce(f32[4,16]{1,0:T(4,128)S(1)} %get-tuple-element.5), channel_id=1, replica_groups=mesh['groups'=2,'seq'=4,'head'=4] {'head'}, use_global_device_ids=true, to_apply=%region_8.9 | all-reduce | flops 64 | bytes 512 | tf_op jit(solution)/shard_map/psum | solution.py:107
  60.1 8.5 %reduce-scatter.2.cloned.1.call-done = f32[4,16,256]{2,1,0:T(8,128)} async-done(((f32[4,16,1024]{2,1,0:T(8,128)}), f32[4,16,256]{2,1,0:T(8,128)}) %reduce-scatter.2.cloned.1.call-update) | async-done | bytes 65552 | tf_op jit(solution)/shard_map/reduce_scatter | solution.py:108
  68.6 1.5 %multiply_convert_fusion = bf16[4,16,256]{2,1,0:T(8,128)(2,1)} fusion(f32[4,16,256]{2,1,0:T(8,128)} %reduce-scatter.2.cloned.1.call-done, f32[4,16]{1,0:T(4,128)S(1)} %add_rsqrt_fusion), kind=kLoop, calls=%fused_computation.41 | loop fusion | flops 32768 | bytes 98560 | tf_op jit(solution)/shard_map/convert_element_type | solution.py:110
  (17 shorter events, 0.2 us)
Async XLA Ops:
  6.5 39.5 %copy-start = (bf16[256,1024]{1,0:T(8,128)(2,1)S(1)}, bf16[256,1024]{1,0:T(8,128)(2,1)}, u32[]{:S(2)}) copy-start(bf16[256,1024]{1,0:T(8,128)(2,1)} %param.25) | copy-start | bytes 1572868
  17.3 11.3 %all-to-all-start = ((f32[4,1,128]{2,1,0:T(1,128)}), f32[4,1,128]{2,1,0:T(1,128)S(1)}, u32[]{:S(2)}, u32[]{:S(2)}) async-start(f32[4,1,128]{2,1,0:T(1,128)} %reshape.128), calls=%async_computation | async-start | bytes 4096 | tf_op jit(solution)/shard_map/all_to_all | solution.py:67
  27.9 18.1 %copy-start.1 = (f32[256]{0:T(256)S(1)}, f32[256]{0:T(256)}, u32[]{:S(2)}) copy-start(f32[256]{0:T(256)} %param.24) | copy-start | bytes 3076
  28.6 7.0 %all-to-all-start.2 = ((f32[4,1,128]{2,1,0:T(1,128)}), f32[4,1,128]{2,1,0:T(1,128)S(1)}, u32[]{:S(2)}, u32[]{:S(2)}) async-start(f32[4,1,128]{2,1,0:T(1,128)} %reshape.130), calls=%async_computation.2 | async-start | bytes 4096 | tf_op jit(solution)/shard_map/all_to_all | solution.py:68
  35.6 9.4 %all-to-all-start.1 = ((f32[1,16,16,2,128]{4,2,3,0,1:T(8,128)}), f32[1,16,16,2,128]{4,2,3,0,1:T(8,128)S(1)}, u32[]{:S(2)}, u32[]{:S(2)}) async-start(f32[1,16,16,2,128]{4,2,3,0,1:T(8,128)} %fusion.13), calls=%async_computation.1 | async-start | bytes 524288 | tf_op jit(solution)/shard_map/all_to_all | solution.py:69
  39.0 29.6 %reduce-scatter.2.cloned.1.call-start = ((), (), s32[]{:S(2)}) async-start(), calls=%async_computation.4 | async-start | bytes 327680 | tf_op jit(solution)/shard_map/reduce_scatter | solution.py:108
Sparse Core Ops, SparseCore 0:
  47.8 20.6 reduce-scatter.1
where the time goes:
time: 77.7 us; the launch traced here: 77 us
  matrix products  16.5 us (21%)
  waiting for transfers between devices  14.3 us (18%)
  between operations  13.5 us (17%)
  blocking collectives  12.4 us (16%)
  starting transfers between devices  11 us (14%)
  other arithmetic  6.4 us (8%)
  local copies, waits for them, and re-layouts  2.82 us (4%)
    psum x1, blocking collectives, body(): squares = lax.psum(local_squares, 'head')  12.4 us
    reduce_scatter x1, waiting for transfers between devices, body(): lax.psum_scatter(partial_out, 'head', scatter_dimension=2, tiled=True)  8.48 us
    dot_general x1, matrix products, body(): jnp.einsum('uchd,ushd->uchs', query_heads, key_heads, preferred_element_t...  5.78 us
    dot_general x1, matrix products, body(): jnp.einsum('uchs,ushd->uchd', weights.astype(jnp.bfloat16), value_heads,...  5.58 us
    all_to_all x1, waiting for transfers between devices, body(): lax.all_to_all(block_acc[None], 'seq', split_axis=1, concat_axis=0, tiled...  4.5 us
    all_to_all x1, starting transfers between devices, body(): lax.all_to_all(block_max[None], 'seq', split_axis=1, concat_axis=0, tiled...  4.26 us
    all_to_all x1, starting transfers between devices, body(): lax.all_to_all(block_acc[None], 'seq', split_axis=1, concat_axis=0, tiled...  3.4 us
    all_to_all x1, starting transfers between devices, body(): lax.all_to_all(block_sum[None], 'seq', split_axis=1, concat_axis=0, tiled...  3.29 us
  transfers between devices with their start and end apart: 4, of which 3 were waited for; matrix products, arithmetic and copies ran while one was open for 14% of the time, Pallas kernels for 0%

commit v1 on v0

v1 whole, which is shorter than its diff:
```python
import functools
import math

import jax
import jax.numpy as jnp
from jax import lax
from jax.experimental import pallas as pl
from jax.experimental.pallas import tpu as pltpu
from jax.sharding import PartitionSpec as P

LANES = 128
SUBLANES = 8
MASKED = -1e30
HALF = LANES // 2


def column_to_row(column, first_lane):
    rows = column.shape[0]
    row_id = lax.broadcasted_iota(jnp.int32, (rows, LANES), 0)
    lane_id = lax.broadcasted_iota(jnp.int32, (rows, LANES), 1)
    return jnp.sum(
        jnp.where(lane_id == row_id + first_lane, column, 0.0), axis=0, keepdims=True
    )


def attend_kernel(
    query_hbm,
    new_key_hbm,
    new_value_hbm,
    keys_hbm,
    values_hbm,
    lengths_hbm,
    time_bucket_hbm,
    action_hbm,
    time_bias_hbm,
    action_bias_hbm,
    gate_hbm,
    gain_hbm,
    packed_ref,
    self_ref,
    gated_ref,
    key_buf,
    value_buf,
    query_buf,
    new_key_buf,
    new_value_buf,
    gate_buf,
    gain_buf,
    bucket_buf,
    action_buf,
    time_table,
    action_table,
    bias_buf,
    lengths_smem,
    block_sems,
    small_sems,
    *,
    unroll,
):
    users, block_len, width = key_buf.shape
    cands = query_buf.shape[1]
    head_count = time_table.shape[0]
    head_size = width // head_count
    group_rows = head_count * cands
    seq_count = packed_ref.shape[0]
    local_users = users // seq_count
    stat_row = local_users * group_rows
    scale = 1.0 / math.sqrt(head_size)
    rank = lax.axis_index("seq")
    first_user = rank * local_users

    small = [
        pltpu.make_async_copy(source, target, small_sems.at[number])
        for number, (source, target) in enumerate(
            [
                (lengths_hbm, lengths_smem),
                (time_bias_hbm, time_table),
                (action_bias_hbm, action_table),
                (time_bucket_hbm, bucket_buf),
                (action_hbm, action_buf),
                (query_hbm, query_buf),
                (new_key_hbm.at[pl.ds(first_user, local_users)], new_key_buf),
                (new_value_hbm.at[pl.ds(first_user, local_users)], new_value_buf),
                (gate_hbm.at[pl.ds(first_user, local_users)], gate_buf),
                (gain_hbm, gain_buf),
            ]
        )
    ]

    def key_copy(user):
        return pltpu.make_async_copy(keys_hbm.at[user], key_buf.at[user], block_sems.at[0, user])

    def value_copy(user):
        return pltpu.make_async_copy(
            values_hbm.at[user], value_buf.at[user], block_sems.at[1, user]
        )

    for copy in small[:6]:
        copy.start()
    for user in range(users):
        key_copy(user).start()
        value_copy(user).start()
    for copy in small[6:]:
        copy.start()
    for copy in small[:6]:
        copy.wait()

    lane_id = lax.broadcasted_iota(jnp.int32, (SUBLANES, LANES), 1)
    sub_id = lax.broadcasted_iota(jnp.int32, (SUBLANES, LANES), 0)

    def padded_table(ref, head):
        row = ref[head : head + 1, :]
        missing = LANES - row.shape[1]
        row = jnp.concatenate([row, jnp.zeros((1, missing), row.dtype)], axis=1)
        return jnp.broadcast_to(row, (SUBLANES, LANES))

    time_rows = [padded_table(time_table, head) for head in range(head_count)]
    action_rows = [padded_table(action_table, head) for head in range(head_count)]
    for group in range(users // SUBLANES):
        limit = jnp.zeros((SUBLANES, LANES), jnp.int32)
        for member in range(SUBLANES):
            left = lengths_smem[group * SUBLANES + member] - rank * block_len
            limit = jnp.where(sub_id == member, left, limit)
        rows = slice(group * SUBLANES, (group + 1) * SUBLANES)
        for piece in range(block_len // LANES):
            cols = slice(piece * LANES, (piece + 1) * LANES)
            bucket = bucket_buf[rows, cols]
            kind = action_buf[rows, cols]
            valid = lane_id + piece * LANES < limit
            for head in range(head_count):
                bias = jnp.take_along_axis(
                    time_rows[head], bucket, axis=1, mode="promise_in_bounds"
                ) + jnp.take_along_axis(
                    action_rows[head], kind, axis=1, mode="promise_in_bounds"
                )
                bias_buf[head, rows, cols] = jnp.where(valid, bias, MASKED)

    col_head = lax.broadcasted_iota(jnp.int32, (cands, width), 1) // head_size

    def one_user(user):
        key_copy(user).wait()
        query = query_buf[user]
        stacked = jnp.concatenate(
            [
                jnp.where(col_head == head, query, jnp.zeros_like(query))
                for head in range(head_count)
            ],
            axis=0,
        )
        scores = lax.dot_general(
            stacked,
            key_buf[user],
            (((1,), (1,)), ((), ())),
            preferred_element_type=jnp.float32,
        )
        biases = jnp.concatenate(
            [
                jnp.broadcast_to(bias_buf[head, pl.ds(user, 1), :], (cands, block_len))
                for head in range(head_count)
            ],
            axis=0,
        )
        scores = scores * scale + biases
        block_max = jnp.max(scores, axis=1, keepdims=True)
        weights = jnp.exp(scores - block_max)
        block_sum = jnp.sum(weights, axis=1, keepdims=True)
        value_copy(user).wait()
        block_acc = jnp.dot(
            weights.astype(jnp.bfloat16), value_buf[user], preferred_element_type=jnp.float32
        )
        target = user // local_users
        place = user % local_users
        for head in range(head_count):
            packed_ref[
                target, pl.ds(pl.multiple_of(place * group_rows + head * cands, SUBLANES), cands), :
            ] = block_acc[
                head * cands : (head + 1) * cands, head * head_size : (head + 1) * head_size
            ]
        packed_ref[target, pl.ds(stat_row + place, 1), :] = column_to_row(
            block_max, 0
        ) + column_to_row(block_sum, HALF)

    def several(step, carry):
        for member in range(unroll):
            one_user(step * unroll + member)
        return carry

    lax.fori_loop(0, users // unroll, several, 0)

    for copy in small[6:]:
        copy.wait()
    gain = gain_buf[...].reshape(1, width)
    for place in range(local_users):
        own_query = query_buf[first_user + place].astype(jnp.float32)
        own_key = new_key_buf[place].astype(jnp.float32)
        own_value = new_value_buf[place].astype(jnp.float32)
        gate = gate_buf[place].astype(jnp.float32)
        product = own_query * own_key
        row = jnp.zeros((1, LANES), jnp.float32)
        for head in range(head_count):
            cols = slice(head * head_size, (head + 1) * head_size)
            own = jnp.sum(product[:, cols], axis=1, keepdims=True) * scale
            row = row + column_to_row(own, head * cands)
            row = row + column_to_row(jnp.ones_like(own), HALF + head * cands)
            first = place * group_rows + head * cands
            self_ref[first : first + cands, :] = own_value[:, cols]
        self_ref[stat_row + place : stat_row + place + 1, :] = row
        gated_ref[place * cands : (place + 1) * cands, :] = gain * (gate / (1.0 + jnp.exp(-gate)))


def project_kernel(packed_ref, self_ref, gated_ref, w_ref, send_ref, *, cands):
    seq_count, _, head_size = packed_ref.shape
    row_count, width = gated_ref.shape
    head_count = width // head_size
    local_users = row_count // cands
    group_rows = head_count * cands
    stat_row = local_users * group_rows
    dest_count, _, out_cols = send_ref.shape
    sources = seq_count + 1

    stats = []
    for place in range(local_users):
        for source in range(seq_count):
            stats.append(packed_ref[source, stat_row + place : stat_row + place + 1, :])
        stats.append(self_ref[stat_row + place : stat_row + place + 1, :])
    missing = LANES - len(stats)
    stats.append(jnp.zeros((missing, LANES), jnp.float32))
    columns = jnp.concatenate(stats, axis=0).T

    hidden = []
    square_row = jnp.zeros((1, LANES), jnp.float32)
    for place in range(local_users):
        span = slice(place * sources, (place + 1) * sources)
        maxima = columns[0:group_rows, span]
        sums = columns[HALF : HALF + group_rows, span]
        top = jnp.max(maxima, axis=1, keepdims=True)
        factors = jnp.exp(maxima - top)
        factors = factors / jnp.sum(factors * sums, axis=1, keepdims=True)
        rows = slice(place * group_rows, (place + 1) * group_rows)
        attended = factors[:, seq_count:] * self_ref[rows, :]
        for source in range(seq_count):
            attended = attended + factors[:, source : source + 1] * packed_ref[source, rows, :]
        wide = jnp.concatenate(
            [attended[head * cands : (head + 1) * cands, :] for head in range(head_count)], axis=1
        )
        square = jnp.sum(wide * wide, axis=1, keepdims=True)
        square_row = square_row + column_to_row(square, place * cands)
        gated = gated_ref[place * cands : (place + 1) * cands, :]
        hidden.append((wide * gated).astype(jnp.bfloat16))
    projected = jnp.dot(
        jnp.concatenate(hidden, axis=0), w_ref[...], preferred_element_type=jnp.float32
    )
    for dest in range(dest_count):
        send_ref[dest, 0:row_count, :] = projected[:, dest * out_cols : (dest + 1) * out_cols]
        send_ref[dest, row_count : row_count + 1, 0:LANES] = square_row


def finish_kernel(parts_ref, out_ref, *, full_width):
    head_axis, _, out_cols = parts_ref.shape
    local_users, cands, _ = out_ref.shape
    row_count = local_users * cands
    total = parts_ref[0, 0:row_count, :]
    square_row = parts_ref[0, row_count : row_count + 1, 0:LANES]
    for source in range(1, head_axis):
        total = total + parts_ref[source, 0:row_count, :]
        square_row = square_row + parts_ref[source, row_count : row_count + 1, 0:LANES]
    row_id = lax.broadcasted_iota(jnp.int32, (row_count, LANES), 0)
    lane_id = lax.broadcasted_iota(jnp.int32, (row_count, LANES), 1)
    squares = jnp.sum(jnp.where(lane_id == row_id, square_row, 0.0), axis=1, keepdims=True)
    factor = 1.0 / jnp.sqrt(squares / full_width + 1e-06)
    result = (total * factor).astype(out_ref.dtype)
    for place in range(local_users):
        out_ref[place] = result[place * cands : (place + 1) * cands, :]


def body(
    query,
    new_key,
    new_value,
    keys,
    values,
    lengths,
    time_bucket,
    action,
    time_bias,
    action_bias,
    gate,
    norm_gain,
    w_out,
):
    users, block_len, width = keys.shape
    cands = query.shape[1]
    head_count = time_bias.shape[1]
    head_size = width // head_count
    seq_count = lax.axis_size("seq")
    head_axis = lax.axis_size("head")
    local_users = users // seq_count
    row_count = local_users * cands
    group_rows = head_count * cands
    packet_rows = local_users * group_rows + SUBLANES
    out_cols = w_out.shape[1] // head_axis
    f32 = jnp.float32
    any_spec = pl.BlockSpec(memory_space=pl.ANY)
    vmem_spec = pl.BlockSpec(memory_space=pltpu.VMEM)

    packed, own, gated = pl.pallas_call(
        functools.partial(attend_kernel, unroll=4),
        out_shape=(
            jax.ShapeDtypeStruct((seq_count, packet_rows, head_size), f32),
            jax.ShapeDtypeStruct((packet_rows, head_size), f32),
            jax.ShapeDtypeStruct((row_count, width), f32),
        ),
        in_specs=[any_spec] * 12,
        out_specs=(vmem_spec, vmem_spec, vmem_spec),
        scratch_shapes=[
            pltpu.VMEM(keys.shape, keys.dtype),
            pltpu.VMEM(values.shape, values.dtype),
            pltpu.VMEM(query.shape, query.dtype),
            pltpu.VMEM((local_users, cands, width), new_key.dtype),
            pltpu.VMEM((local_users, cands, width), new_value.dtype),
            pltpu.VMEM((local_users, cands, width), gate.dtype),
            pltpu.VMEM(norm_gain.shape, f32),
            pltpu.VMEM(time_bucket.shape, jnp.int32),
            pltpu.VMEM(action.shape, jnp.int32),
            pltpu.VMEM(time_bias.shape[::-1], f32),
            pltpu.VMEM(action_bias.shape[::-1], f32),
            pltpu.VMEM((head_count, users, block_len), f32),
            pltpu.SMEM(lengths.shape, jnp.int32),
            pltpu.SemaphoreType.DMA((2, users)),
            pltpu.SemaphoreType.DMA((10,)),
        ],
        name="attend",
    )(
        query,
        new_key,
        new_value,
        keys,
        values,
        lengths,
        time_bucket,
        action,
        time_bias.T,
        action_bias.T,
        gate,
        norm_gain,
    )
    received = lax.all_to_all(packed, "seq", split_axis=0, concat_axis=0, tiled=True)
    sent = pl.pallas_call(
        functools.partial(project_kernel, cands=cands),
        out_shape=jax.ShapeDtypeStruct((head_axis, row_count + SUBLANES, out_cols), f32),
        in_specs=[vmem_spec] * 4,
        out_specs=vmem_spec,
        name="project",
    )(received, own, gated, w_out)
    parts = lax.all_to_all(sent, "head", split_axis=0, concat_axis=0, tiled=True)
    return pl.pallas_call(
        functools.partial(finish_kernel, full_width=width * head_axis),
        out_shape=jax.ShapeDtypeStruct((local_users, cands, out_cols), jnp.bfloat16),
        in_specs=[vmem_spec],
        out_specs=vmem_spec,
        name="finish",
    )(parts)


def solution(mesh):
    placed = (
        P("groups", None, "head"),
        P("groups", None, "head"),
        P("groups", None, "head"),
        P("groups", "seq", "head"),
        P("groups", "seq", "head"),
        P("groups"),
        P("groups", "seq"),
        P("groups", "seq"),
        P(None, "head"),
        P(None, "head"),
        P("groups", None, "head"),
        P("head"),
        P("head", None),
    )
    return jax.shard_map(
        body,
        mesh=mesh,
        in_specs=placed,
        out_specs=P(("groups", "seq"), None, "head"),
        check_vma=False,
    )
```

time: 77.7 us -> 49.8 us (0.64)
  Pallas kernels: 0 us -> 22.8 us
  matrix products: 16.5 us -> 0 us
  waiting for transfers between devices: 14.3 us -> 0 us
  blocking collectives: 12.4 us -> 26.6 us
  between operations: 13.5 us -> 0.01 us
  starting transfers between devices: 11 us -> 0 us
  other arithmetic: 6.4 us -> 0 us
  local copies, waits for them, and re-layouts: 2.82 us -> 0 us
    all_to_all x0 -> x2, blocking collectives: none -> 26.6 us  [the longest x1 15.5 us: body(): lax.all_to_all(sent, 'head', split_axis=0, concat_axis=0, tiled=True)]
    pallas_call x0 -> x3, Pallas kernels: none -> 22.8 us  [the longest x1 18.6 us: body(): pl.pallas_call(functools.partial(attend_kernel, unroll=4), out_shape=(jax...]
    dot_general x5 -> x0, matrix products: 16.5 us -> none  [the longest x1 5.78 us: body(): jnp.einsum('uchd,ushd->uchs', query_heads, key_heads, preferred_element_t...]
    psum x1 -> x0, blocking collectives: 12.4 us -> none  [body(): squares = lax.psum(local_squares, 'head')]
    all_to_all x3 -> x0, starting transfers between devices: 11 us -> none  [the longest x1 4.26 us: body(): lax.all_to_all(block_max[None], 'seq', split_axis=1, concat_axis=0, tiled...]
    reduce_scatter x1 -> x0, waiting for transfers between devices: 8.48 us -> none  [body(): lax.psum_scatter(partial_out, 'head', scatter_dimension=2, tiled=True)]
    all_to_all x3 -> x0, waiting for transfers between devices: 5.82 us -> none  [the longest x1 4.5 us: body(): lax.all_to_all(block_acc[None], 'seq', split_axis=1, concat_axis=0, tiled...]
    reduce_sum x5 -> x0, other arithmetic: 1.98 us -> none  [the longest x1 0.93 us: body(): local_squares = jnp.sum(jnp.square(attended), axis=(2, 3))]
  transfers between devices with their start and end apart: 4 -> 0, of which waited for: 3 -> 0; matrix products, arithmetic and copies ran while one was open for 14% -> 0% of each run, Pallas kernels for 0% -> 0%
where the time goes in v1:
time: 49.8 us; the launch traced here: 49.4 us
  blocking collectives  26.6 us (53%)
  Pallas kernels  22.8 us (46%)
    pallas_call x1, Pallas kernels, body(): pl.pallas_call(functools.partial(attend_kernel, unroll=4), out_shape=(jax...  18.6 us
    all_to_all x1, blocking collectives, body(): lax.all_to_all(sent, 'head', split_axis=0, concat_axis=0, tiled=True)  15.5 us
    all_to_all x1, blocking collectives, body(): lax.all_to_all(packed, 'seq', split_axis=0, concat_axis=0, tiled=True)  11 us
    pallas_call x1, Pallas kernels, body(): pl.pallas_call(functools.partial(project_kernel, cands=cands), out_shape=...  2.54 us
    pallas_call x1, Pallas kernels, body(): pl.pallas_call(functools.partial(finish_kernel, full_width=width * head_a...  1.68 us

profile of v1, /device:TPU:0, one launch (start us, length us, event | category | flops | bytes accessed | tf_op | source)
XLA Modules:
  0.0 49.4 jit_solution(15707077491494281058)
XLA Ops:
  0.0 18.6 %attend.1 = (f32[4,136,128]{2,1,0:T(8,128)}, f32[136,128]{1,0:T(8,128)}, f32[64,256]{1,0:T(8,128)}) custom-call(bf16[16,16,256]{2,1,0:T(8,128)(2,1)} %query_hbm.1, bf16[16,16,256]{2,1,0:T(8,128)(2,1)} %new_key_hbm.1, bf16[16,16,256]{2,1,0:T(8,128)(2,1)} %new_value_hbm.1, bf16[16,1024,256]{2,1,0:T(8,128)(2,1)} %keys_hbm.1, bf16[16,1024,256]{2,1,0:T(8,128)(2,1)} %values_hbm.1, ...), custom_call_target="tpu_custom_call" | custom-call | tf_op jit(solution)/shard_map/attend/pallas_call | solution.py:306
  18.6 11.0 %all_to_all.10.packed_ref = f32[4,136,128]{2,1,0:T(8,128)} all-to-all(f32[4,136,128]{2,1,0:T(8,128)} %get-tuple-element.8), channel_id=1, replica_groups=mesh['groups'=2,'seq'=4,'head'=4] {'seq'}, dimensions={0} | all-to-all | bytes 557056 | tf_op jit(solution)/shard_map/all_to_all | solution.py:347
  29.7 2.5 %project.1 = f32[4,72,256]{2,1,0:T(8,128)} custom-call(f32[4,136,128]{2,1,0:T(8,128)} %all_to_all.10.packed_ref, f32[136,128]{1,0:T(8,128)} %get-tuple-element.9.self_ref, f32[64,256]{1,0:T(8,128)} %get-tuple-element.10.gated_ref, bf16[256,1024]{1,0:T(8,128)(2,1)} %w_ref.1), custom_call_target="tpu_custom_call" | custom-call | tf_op jit(solution)/shard_map/project/pallas_call | solution.py:348
  32.2 15.5 %all_to_all.11.parts_ref = f32[4,72,256]{2,1,0:T(8,128)} all-to-all(f32[4,72,256]{2,1,0:T(8,128)} %project.1), channel_id=1, replica_groups=mesh['groups'=2,'seq'=4,'head'=4] {'head'}, dimensions={0} | all-to-all | bytes 589824 | tf_op jit(solution)/shard_map/all_to_all | solution.py:355
  47.8 1.7 %finish.1 = bf16[4,16,256]{2,1,0:T(8,128)(2,1)} custom-call(f32[4,72,256]{2,1,0:T(8,128)} %all_to_all.11.parts_ref), custom_call_target="tpu_custom_call" | custom-call | tf_op jit(solution)/shard_map/finish/pallas_call | solution.py:356

commit v2 on v1

v2 whole, which is shorter than its diff:
```python
import functools
import math

import jax
import jax.numpy as jnp
from jax import lax
from jax.experimental import pallas as pl
from jax.experimental.pallas import tpu as pltpu
from jax.sharding import PartitionSpec as P

LANES = 128
SUBLANES = 8
MASKED = -1e30
HALF = LANES // 2
STEP_USERS = 4
AHEAD = 2
SPLIT = False


def partner_of(rank, offset, size):
    if size & (size - 1) == 0:
        return rank ^ offset
    return (rank + offset) % size


def exchange(packet, axis, offset):
    size = lax.axis_size(axis)
    pairs = [(rank, partner_of(rank, offset, size)) for rank in range(size)]
    return lax.ppermute(packet, axis, pairs)


def column_to_row(column, first_lane):
    rows = column.shape[0]
    row_id = lax.broadcasted_iota(jnp.int32, (rows, LANES), 0)
    lane_id = lax.broadcasted_iota(jnp.int32, (rows, LANES), 1)
    return jnp.sum(
        jnp.where(lane_id == row_id + first_lane, column, 0.0), axis=0, keepdims=True
    )


def attend_kernel(*refs, offsets, seq_count, with_own, step_users, ahead):
    refs = list(refs)
    take = lambda count: [refs.pop(0) for _ in range(count)]
    (
        query_hbm,
        keys_hbm,
        values_hbm,
        lengths_hbm,
        time_bucket_hbm,
        action_hbm,
        time_bias_hbm,
        action_bias_hbm,
    ) = take(8)
    if with_own:
        new_key_hbm, new_value_hbm, gate_hbm, gain_hbm = take(4)
    packets = take(len(offsets))
    if with_own:
        self_ref, gated_ref = take(2)
    (
        key_buf,
        value_buf,
        query_buf,
        bucket_buf,
        action_buf,
        time_table,
        action_table,
        bias_buf,
        lengths_smem,
        block_sems,
        small_sems,
    ) = take(11)
    if with_own:
        new_key_buf, new_value_buf, gate_buf, gain_buf, own_sems = take(5)
    _, block_len, width = key_buf.shape
    users, cands, _ = query_buf.shape
    head_count = time_table.shape[0]
    head_size = width // head_count
    group_rows = head_count * cands
    local_users = users // seq_count
    stat_row = local_users * group_rows
    scale = 1.0 / math.sqrt(head_size)
    rank = lax.axis_index("seq")
    first_user = rank * local_users

    small = [
        pltpu.make_async_copy(source, target, small_sems.at[number])
        for number, (source, target) in enumerate(
            [
                (lengths_hbm, lengths_smem),
                (time_bias_hbm, time_table),
                (action_bias_hbm, action_table),
                (time_bucket_hbm, bucket_buf),
                (action_hbm, action_buf),
                (query_hbm, query_buf),
            ]
        )
    ]
    late = []
    if with_own:
        own_rows = pl.ds(first_user, local_users)
        late = [
            pltpu.make_async_copy(source, target, own_sems.at[number])
            for number, (source, target) in enumerate(
                [
                    (new_key_hbm.at[own_rows], new_key_buf),
                    (new_value_hbm.at[own_rows], new_value_buf),
                    (gate_hbm.at[own_rows], gate_buf),
                    (gain_hbm, gain_buf),
                ]
            )
        ]

    steps = [
        (slot, place)
        for slot in range(len(offsets))
        for place in range(0, local_users, step_users)
    ]

    def copies(number):
        slot, place = steps[number]
        source = pl.ds(
            partner_of(rank, offsets[slot], seq_count) * local_users + place, step_users
        )
        target = pl.ds(number * step_users, step_users)
        return (
            pltpu.make_async_copy(
                keys_hbm.at[source], key_buf.at[target], block_sems.at[0, number]
            ),
            pltpu.make_async_copy(
                values_hbm.at[source], value_buf.at[target], block_sems.at[1, number]
            ),
        )

    for copy in small:
        copy.start()
    for number in range(min(ahead, len(steps))):
        for copy in copies(number):
            copy.start()
    for copy in late:
        copy.start()
    for copy in small:
        copy.wait()

    lane_id = lax.broadcasted_iota(jnp.int32, (SUBLANES, LANES), 1)
    sub_id = lax.broadcasted_iota(jnp.int32, (SUBLANES, LANES), 0)

    def padded_table(ref, head):
        row = ref[head : head + 1, :]
        missing = LANES - row.shape[1]
        row = jnp.concatenate([row, jnp.zeros((1, missing), row.dtype)], axis=1)
        return jnp.broadcast_to(row, (SUBLANES, LANES))

    time_rows = [padded_table(time_table, head) for head in range(head_count)]
    action_rows = [padded_table(action_table, head) for head in range(head_count)]
    for group in range(users // SUBLANES):
        limit = jnp.zeros((SUBLANES, LANES), jnp.int32)
        for member in range(SUBLANES):
            left = lengths_smem[group * SUBLANES + member] - rank * block_len
            limit = jnp.where(sub_id == member, left, limit)
        rows = slice(group * SUBLANES, (group + 1) * SUBLANES)
        for piece in range(block_len // LANES):
            cols = slice(piece * LANES, (piece + 1) * LANES)
            bucket = bucket_buf[rows, cols]
            kind = action_buf[rows, cols]
            valid = lane_id + piece * LANES < limit
            for head in range(head_count):
                bias = jnp.take_along_axis(
                    time_rows[head], bucket, axis=1, mode="promise_in_bounds"
                ) + jnp.take_along_axis(
                    action_rows[head], kind, axis=1, mode="promise_in_bounds"
                )
                bias_buf[head, rows, cols] = jnp.where(valid, bias, MASKED)

    col_head = lax.broadcasted_iota(jnp.int32, (cands, width), 1) // head_size

    def one_user(slot, place, held):
        user = partner_of(rank, offsets[slot], seq_count) * local_users + place
        query = query_buf[user]
        stacked = jnp.concatenate(
            [
                jnp.where(col_head == head, query, jnp.zeros_like(query))
                for head in range(head_count)
            ],
            axis=0,
        )
        scores = lax.dot_general(
            stacked,
            key_buf[held],
            (((1,), (1,)), ((), ())),
            preferred_element_type=jnp.float32,
        )
        biases = jnp.concatenate(
            [
                jnp.broadcast_to(bias_buf[head, pl.ds(user, 1), :], (cands, block_len))
                for head in range(head_count)
            ],
            axis=0,
        )
        scores = scores * scale + biases
        block_max = jnp.max(scores, axis=1, keepdims=True)
        weights = jnp.exp(scores - block_max)
        block_sum = jnp.sum(weights, axis=1, keepdims=True)
        block_acc = jnp.dot(
            weights.astype(jnp.bfloat16), value_buf[held], preferred_element_type=jnp.float32
        )
        packet = packets[slot]
        for head in range(head_count):
            first = place * group_rows + head * cands
            packet[first : first + cands, :] = block_acc[
                head * cands : (head + 1) * cands, head * head_size : (head + 1) * head_size
            ]
        packet[stat_row + place : stat_row + place + 1, :] = column_to_row(
            block_max, 0
        ) + column_to_row(block_sum, HALF)

    for number, (slot, place) in enumerate(steps):
        for copy in copies(number):
            copy.wait()
        if number + ahead < len(steps):
            for copy in copies(number + ahead):
                copy.start()
        for member in range(step_users):
            one_user(slot, place + member, number * step_users + member)

    if not with_own:
        return
    for copy in late:
        copy.wait()
    gain = gain_buf[...].reshape(1, width)
    for place in range(local_users):
        own_query = query_buf[first_user + place].astype(jnp.float32)
        own_key = new_key_buf[place].astype(jnp.float32)
        own_value = new_value_buf[place].astype(jnp.float32)
        gate = gate_buf[place].astype(jnp.float32)
        product = own_query * own_key
        row = jnp.zeros((1, LANES), jnp.float32)
        for head in range(head_count):
            cols = slice(head * head_size, (head + 1) * head_size)
            own = jnp.sum(product[:, cols], axis=1, keepdims=True) * scale
            row = row + column_to_row(own, head * cands)
            row = row + column_to_row(jnp.ones_like(own), HALF + head * cands)
            first = place * group_rows + head * cands
            self_ref[first : first + cands, :] = own_value[:, cols]
        self_ref[stat_row + place : stat_row + place + 1, :] = row
        gated_ref[place * cands : (place + 1) * cands, :] = gain * (gate / (1.0 + jnp.exp(-gate)))


def project_kernel(*refs, cands, source_count, head_axis):
    packets = refs[:source_count]
    gated_ref, w_ref = refs[source_count : source_count + 2]
    sends = refs[source_count + 2 :]
    head_size = packets[0].shape[1]
    row_count, width = gated_ref.shape
    head_count = width // head_size
    local_users = row_count // cands
    group_rows = head_count * cands
    stat_row = local_users * group_rows
    out_cols = w_ref.shape[1] // head_axis
    rank = lax.axis_index("head")

    stats = [
        packet[stat_row + place : stat_row + place + 1, :]
        for place in range(local_users)
        for packet in packets
    ]
    stats.append(jnp.zeros((LANES - len(stats), LANES), jnp.float32))
    columns = jnp.concatenate(stats, axis=0).T

    hidden = []
    square_row = jnp.zeros((1, LANES), jnp.float32)
    for place in range(local_users):
        span = slice(place * source_count, (place + 1) * source_count)
        maxima = columns[0:group_rows, span]
        sums = columns[HALF : HALF + group_rows, span]
        top = jnp.max(maxima, axis=1, keepdims=True)
        factors = jnp.exp(maxima - top)
        factors = factors / jnp.sum(factors * sums, axis=1, keepdims=True)
        rows = slice(place * group_rows, (place + 1) * group_rows)
        attended = factors[:, 0:1] * packets[0][rows, :]
        for source in range(1, source_count):
            attended = attended + factors[:, source : source + 1] * packets[source][rows, :]
        wide = jnp.concatenate(
            [attended[head * cands : (head + 1) * cands, :] for head in range(head_count)], axis=1
        )
        square = jnp.sum(wide * wide, axis=1, keepdims=True)
        square_row = square_row + column_to_row(square, place * cands)
        gated = gated_ref[place * cands : (place + 1) * cands, :]
        hidden.append((wide * gated).astype(jnp.bfloat16))
    hidden = jnp.concatenate(hidden, axis=0)
    for offset in reversed(range(head_axis)):
        first = pl.multiple_of(partner_of(rank, offset, head_axis) * out_cols, LANES)
        sends[offset][0:row_count, :] = jnp.dot(
            hidden, w_ref[:, pl.ds(first, out_cols)], preferred_element_type=jnp.float32
        )
        sends[offset][row_count : row_count + 1, 0:LANES] = square_row


def finish_kernel(*refs, full_width):
    parts, out_ref = refs[:-1], refs[-1]
    local_users, cands, _ = out_ref.shape
    row_count = local_users * cands
    total = parts[0][0:row_count, :]
    square_row = parts[0][row_count : row_count + 1, 0:LANES]
    for part in parts[1:]:
        total = total + part[0:row_count, :]
        square_row = square_row + part[row_count : row_count + 1, 0:LANES]
    row_id = lax.broadcasted_iota(jnp.int32, (row_count, LANES), 0)
    lane_id = lax.broadcasted_iota(jnp.int32, (row_count, LANES), 1)
    squares = jnp.sum(jnp.where(lane_id == row_id, square_row, 0.0), axis=1, keepdims=True)
    factor = 1.0 / jnp.sqrt(squares / full_width + 1e-06)
    result = (total * factor).astype(out_ref.dtype)
    for place in range(local_users):
        out_ref[place] = result[place * cands : (place + 1) * cands, :]


def body(
    query,
    new_key,
    new_value,
    keys,
    values,
    lengths,
    time_bucket,
    action,
    time_bias,
    action_bias,
    gate,
    norm_gain,
    w_out,
):
    users, block_len, width = keys.shape
    cands = query.shape[1]
    head_count = time_bias.shape[1]
    head_size = width // head_count
    seq_count = lax.axis_size("seq")
    head_axis = lax.axis_size("head")
    local_users = users // seq_count
    row_count = local_users * cands
    packet_rows = local_users * head_count * cands + SUBLANES
    out_cols = w_out.shape[1] // head_axis
    f32 = jnp.float32
    hbm_spec = pl.BlockSpec(memory_space=pltpu.HBM)
    vmem_spec = pl.BlockSpec(memory_space=pltpu.VMEM)
    packet_shape = jax.ShapeDtypeStruct((packet_rows, head_size), f32)
    step_users = math.gcd(local_users, STEP_USERS)

    def attend(offsets, with_own):
        held = len(offsets) * local_users
        steps = held // step_users
        held_bytes = 2 * held * block_len * width * keys.dtype.itemsize
        operands = [
            query, keys, values, lengths, time_bucket, action, time_bias.T, action_bias.T
        ]
        outputs = [packet_shape] * len(offsets)
        scratch = [
            pltpu.VMEM((held, block_len, width), keys.dtype),
            pltpu.VMEM((held, block_len, width), values.dtype),
            pltpu.VMEM(query.shape, query.dtype),
            pltpu.VMEM(time_bucket.shape, jnp.int32),
            pltpu.VMEM(action.shape, jnp.int32),
            pltpu.VMEM(time_bias.shape[::-1], f32),
            pltpu.VMEM(action_bias.shape[::-1], f32),
            pltpu.VMEM((head_count, users, block_len), f32),
            pltpu.SMEM(lengths.shape, jnp.int32),
            pltpu.SemaphoreType.DMA((2, steps)),
            pltpu.SemaphoreType.DMA((6,)),
        ]
        if with_own:
            operands += [new_key, new_value, gate, norm_gain]
            outputs += [packet_shape, jax.ShapeDtypeStruct((row_count, width), f32)]
            scratch += [
                pltpu.VMEM((local_users, cands, width), new_key.dtype),
                pltpu.VMEM((local_users, cands, width), new_value.dtype),
                pltpu.VMEM((local_users, cands, width), gate.dtype),
                pltpu.VMEM(norm_gain.shape, f32),
                pltpu.SemaphoreType.DMA((4,)),
            ]
        return pl.pallas_call(
            functools.partial(
                attend_kernel,
                offsets=offsets,
                seq_count=seq_count,
                with_own=with_own,
                step_users=step_users,
                ahead=AHEAD,
            ),
            out_shape=tuple(outputs),
            in_specs=[hbm_spec] * len(operands),
            out_specs=tuple([vmem_spec] * len(outputs)),
            scratch_shapes=scratch,
            compiler_params=pltpu.CompilerParams(vmem_limit_bytes=held_bytes + (8 << 20)),
            name="attend",
        )(*[pltpu.with_memory_space_constraint(operand, pltpu.HBM) for operand in operands])

    order = list(reversed(range(seq_count)))
    cut = len(order) // 2 if SPLIT else 0
    received = []
    for offsets, with_own in ((order[:cut], False), (order[cut:], True)):
        if not offsets:
            continue
        results = attend(tuple(offsets), with_own)
        for offset, packet in zip(offsets, results):
            received.append(exchange(packet, "seq", offset) if offset else packet)
        if with_own:
            received.append(results[len(offsets)])
            gated = results[len(offsets) + 1]
    sends = pl.pallas_call(
        functools.partial(
            project_kernel, cands=cands, source_count=len(received), head_axis=head_axis
        ),
        out_shape=tuple(
            [jax.ShapeDtypeStruct((row_count + SUBLANES, out_cols), f32)] * head_axis
        ),
        in_specs=[vmem_spec] * (len(received) + 2),
        out_specs=tuple([vmem_spec] * head_axis),
        compiler_params=pltpu.CompilerParams(vmem_limit_bytes=8 << 20),
        name="project",
    )(*received, gated, w_out)
    parts = [
        exchange(sends[offset], "head", offset) if offset else sends[offset]
        for offset in reversed(range(head_axis))
    ]
    return pl.pallas_call(
        functools.partial(finish_kernel, full_width=width * head_axis),
        out_shape=jax.ShapeDtypeStruct((local_users, cands, out_cols), jnp.bfloat16),
        in_specs=[vmem_spec] * head_axis,
        out_specs=vmem_spec,
        compiler_params=pltpu.CompilerParams(vmem_limit_bytes=4 << 20),
        name="finish",
    )(*parts)


def solution(mesh):
    placed = (
        P("groups", None, "head"),
        P("groups", None, "head"),
        P("groups", None, "head"),
        P("groups", "seq", "head"),
        P("groups", "seq", "head"),
        P("groups"),
        P("groups", "seq"),
        P("groups", "seq"),
        P(None, "head"),
        P(None, "head"),
        P("groups", None, "head"),
        P("head"),
        P("head", None),
    )
    return jax.shard_map(
        body,
        mesh=mesh,
        in_specs=placed,
        out_specs=P(("groups", "seq"), None, "head"),
        check_vma=False,
    )
```

time: 49.8 us -> 29.8 us (0.60)
  blocking collectives: 26.6 us -> 0 us
  Pallas kernels: 22.8 us -> 12 us
  waiting for transfers between devices: 0 us -> 9.86 us
  starting transfers between devices: 0 us -> 7.74 us
    all_to_all x2 -> x0, blocking collectives: 26.6 us -> none  [the longest x1 15.5 us: body(): lax.all_to_all(sent, 'head', split_axis=0, concat_axis=0, tiled=True)]
    pallas_call x2, Pallas kernels: 21.2 us -> 11.3 us  [the longest x1 10.6 us: attend(): pl.pallas_call(functools.partial(attend_kernel, offsets=offsets, seq_coun...]
    ppermute x0 -> x6, waiting for transfers between devices: none -> 9.86 us  [exchange(): return lax.ppermute(packet, axis, pairs)]
    ppermute x0 -> x6, starting transfers between devices: none -> 7.74 us  [exchange(): return lax.ppermute(packet, axis, pairs)]
    pallas_call x1, Pallas kernels: 1.68 us -> 0.73 us  [body(): pl.pallas_call(functools.partial(finish_kernel, full_width=width * head_a...]
  transfers between devices with their start and end apart: 0 -> 6, of which waited for: 0 -> 4; matrix products, arithmetic and copies ran while one was open for 0% -> 0% of each run, Pallas kernels for 0% -> 0%
where the time goes in v2:
time: 29.8 us; the launch traced here: 29.6 us
  Pallas kernels  12 us (40%)
  waiting for transfers between devices  9.86 us (33%)
  starting transfers between devices  7.74 us (26%)
    pallas_call x1, Pallas kernels, attend(): pl.pallas_call(functools.partial(attend_kernel, offsets=offsets, seq_coun...  10.6 us
    ppermute x6, waiting for transfers between devices, exchange(): return lax.ppermute(packet, axis, pairs)  9.86 us
    ppermute x6, starting transfers between devices, exchange(): return lax.ppermute(packet, axis, pairs)  7.74 us
    pallas_call x1, Pallas kernels, body(): pl.pallas_call(functools.partial(finish_kernel, full_width=width * head_a...  0.73 us
    pallas_call x1, Pallas kernels, body(): pl.pallas_call(functools.partial(project_kernel, cands=cands, source_coun...  0.64 us
  transfers between devices with their start and end apart: 6, of which 4 were waited for; matrix products, arithmetic and copies ran while one was open for 0% of the time, Pallas kernels for 0%

profile of v2, /device:TPU:0, one launch (start us, length us, event | category | flops | bytes accessed | tf_op | source)
XLA Modules:
  0.0 29.6 jit_solution(4257513450199761306)
XLA Ops:
  0.0 0.0 copy-start
  0.0 10.6 %attend.1 = (f32[136,128]{1,0:T(8,128)S(1)}, f32[136,128]{1,0:T(8,128)S(1)}, f32[136,128]{1,0:T(8,128)S(1)}, f32[136,128]{1,0:T(8,128)S(1)}, f32[136,128]{1,0:T(8,128)S(1)}, /*index=5*/f32[64,256]{1,0:T(8,128)S(1)}) custom-call(bf16[16,16,256]{2,1,0:T(8,128)(2,1)} %refs_0_.1, bf16[16,1024,256]{2,1,0:T(8,128)(2,1)} %refs_1_.1, ...), custom_call_target="tpu_custom_call" | custom-call | tf_op jit(solution)/shard_map/attend/pallas_call | solution.py:378
  10.6 2.5 %collective-permute-start = (f32[136,128]{1,0:T(8,128)S(1)}, f32[136,128]{1,0:T(8,128)S(1)}, u32[]{:S(2)}, u32[]{:S(2)}) collective-permute-start(f32[136,128]{1,0:T(8,128)S(1)} %get-tuple-element.15), channel_id=1, source_target_pairs={{0,12},{4,8},{8,4},{12,0},{1,13},{5,9},{9,5},{13,1},{2,14},{6,10},... | collective-permute-start | bytes 208904 | tf_op jit(solution)/shard_map/ppermute | solution.py:29
  13.1 0.6 %collective-permute-start.1 = (f32[136,128]{1,0:T(8,128)S(1)}, f32[136,128]{1,0:T(8,128)S(1)}, u32[]{:S(2)}, u32[]{:S(2)}) collective-permute-start(f32[136,128]{1,0:T(8,128)S(1)} %get-tuple-element.16), channel_id=1, source_target_pairs={{0,8},{4,12},{8,0},{12,4},{1,9},{5,13},{9,1},{13,5},{2,10},{6,14},... | collective-permute-start | bytes 208904 | tf_op jit(solution)/shard_map/ppermute | solution.py:29
  13.8 0.0 collective-permute-start.2
  13.8 1.9 %collective-permute-done.refs_0_ = f32[136,128]{1,0:T(8,128)S(1)} collective-permute-done((f32[136,128]{1,0:T(8,128)S(1)}, f32[136,128]{1,0:T(8,128)S(1)}, u32[]{:S(2)}, u32[]{:S(2)}) %collective-permute-start) | collective-permute-done | bytes 69664 | tf_op jit(solution)/shard_map/ppermute | solution.py:29
  15.7 2.2 %collective-permute-done.1.refs_1_ = f32[136,128]{1,0:T(8,128)S(1)} collective-permute-done((f32[136,128]{1,0:T(8,128)S(1)}, f32[136,128]{1,0:T(8,128)S(1)}, u32[]{:S(2)}, u32[]{:S(2)}) %collective-permute-start.1) | collective-permute-done | bytes 69664 | tf_op jit(solution)/shard_map/ppermute | solution.py:29
  17.9 0.0 collective-permute-done.2.refs_2_
  17.9 0.0 copy-done
  17.9 0.6 %project.1 = (f32[72,256]{1,0:T(8,128)S(1)}, f32[72,256]{1,0:T(8,128)S(1)}, f32[72,256]{1,0:T(8,128)S(1)}, f32[72,256]{1,0:T(8,128)S(1)}) custom-call(f32[136,128]{1,0:T(8,128)S(1)} %collective-permute-done.refs_0_, f32[136,128]{1,0:T(8,128)S(1)} %collective-permute-done.1.refs_1_, f32[136,128]{1,0:T(8,128)S(1)} %collective-permute-done.2.refs_2_, ...), custom_call_target="tpu_custom_call" | custom-call | tf_op jit(solution)/shard_map/project/pallas_call | solution.py:407
  18.6 3.9 %collective-permute-start.3 = (f32[72,256]{1,0:T(8,128)S(1)}, f32[72,256]{1,0:T(8,128)S(1)}, u32[]{:S(2)}, u32[]{:S(2)}) collective-permute-start(f32[72,256]{1,0:T(8,128)S(1)} %get-tuple-element.21), channel_id=1, source_target_pairs={{0,3},{1,2},{2,1},{3,0},{4,7},{5,6},{6,5},{7,4},{8,11},{9,10},{10,... | collective-permute-start | bytes 221192 | tf_op jit(solution)/shard_map/ppermute | solution.py:29
  22.5 0.0 collective-permute-start.4
  22.5 0.6 %collective-permute-start.5 = (f32[72,256]{1,0:T(8,128)S(1)}, f32[72,256]{1,0:T(8,128)S(1)}, u32[]{:S(2)}, u32[]{:S(2)}) collective-permute-start(f32[72,256]{1,0:T(8,128)S(1)} %get-tuple-element.23), channel_id=1, source_target_pairs={{0,1},{1,0},{2,3},{3,2},{4,5},{5,4},{6,7},{7,6},{8,9},{9,8},{10,11... | collective-permute-start | bytes 221192 | tf_op jit(solution)/shard_map/ppermute | solution.py:29
  23.1 2.2 %collective-permute-done.3.refs_0_ = f32[72,256]{1,0:T(8,128)S(1)} collective-permute-done((f32[72,256]{1,0:T(8,128)S(1)}, f32[72,256]{1,0:T(8,128)S(1)}, u32[]{:S(2)}, u32[]{:S(2)}) %collective-permute-start.3) | collective-permute-done | bytes 73760 | tf_op jit(solution)/shard_map/ppermute | solution.py:29
  25.3 3.6 %collective-permute-done.4.refs_1_ = f32[72,256]{1,0:T(8,128)S(1)} collective-permute-done((f32[72,256]{1,0:T(8,128)S(1)}, f32[72,256]{1,0:T(8,128)S(1)}, u32[]{:S(2)}, u32[]{:S(2)}) %collective-permute-start.4) | collective-permute-done | bytes 73760 | tf_op jit(solution)/shard_map/ppermute | solution.py:29
  28.9 0.0 collective-permute-done.5.refs_2_
  28.9 0.7 %finish.1 = bf16[4,16,256]{2,1,0:T(8,128)(2,1)} custom-call(f32[72,256]{1,0:T(8,128)S(1)} %collective-permute-done.3.refs_0_, f32[72,256]{1,0:T(8,128)S(1)} %collective-permute-done.4.refs_1_, f32[72,256]{1,0:T(8,128)S(1)} %collective-permute-done.5.refs_2_, f32[72,256]{1,0:T(8,128)S(1)} %get-tuple-element.24.refs_3_), custom_call_target="tpu_custom_call" | custom-call | tf_op jit(solution)/shard_map/finish/pallas_call | solution.py:423
Async XLA Ops:
  0.0 17.9 %copy-start = (bf16[256,1024]{1,0:T(8,128)(2,1)S(1)}, bf16[256,1024]{1,0:T(8,128)(2,1)}, u32[]{:S(2)}) copy-start(bf16[256,1024]{1,0:T(8,128)(2,1)} %refs_6_.1) | copy-start | bytes 1572868
  10.6 5.1 %collective-permute-start = (f32[136,128]{1,0:T(8,128)S(1)}, f32[136,128]{1,0:T(8,128)S(1)}, u32[]{:S(2)}, u32[]{:S(2)}) collective-permute-start(f32[136,128]{1,0:T(8,128)S(1)} %get-tuple-element.15), channel_id=1, source_target_pairs={{0,12},{4,8},{8,4},{12,0},{1,13},{5,9},{9,5},{13,1},{2,14},{6,10},... | collective-permute-start | bytes 208904 | tf_op jit(solution)/shard_map/ppermute | solution.py:29
  13.1 4.8 %collective-permute-start.1 = (f32[136,128]{1,0:T(8,128)S(1)}, f32[136,128]{1,0:T(8,128)S(1)}, u32[]{:S(2)}, u32[]{:S(2)}) collective-permute-start(f32[136,128]{1,0:T(8,128)S(1)} %get-tuple-element.16), channel_id=1, source_target_pairs={{0,8},{4,12},{8,0},{12,4},{1,9},{5,13},{9,1},{13,5},{2,10},{6,14},... | collective-permute-start | bytes 208904 | tf_op jit(solution)/shard_map/ppermute | solution.py:29
  13.8 4.1 %collective-permute-start.2 = (f32[136,128]{1,0:T(8,128)S(1)}, f32[136,128]{1,0:T(8,128)S(1)}, u32[]{:S(2)}, u32[]{:S(2)}) collective-permute-start(f32[136,128]{1,0:T(8,128)S(1)} %get-tuple-element.17), channel_id=1, source_target_pairs={{0,4},{4,0},{8,12},{12,8},{1,5},{5,1},{9,13},{13,9},{2,6},{6,2},{1... | collective-permute-start | bytes 208904 | tf_op jit(solution)/shard_map/ppermute | solution.py:29
  18.6 6.7 %collective-permute-start.3 = (f32[72,256]{1,0:T(8,128)S(1)}, f32[72,256]{1,0:T(8,128)S(1)}, u32[]{:S(2)}, u32[]{:S(2)}) collective-permute-start(f32[72,256]{1,0:T(8,128)S(1)} %get-tuple-element.21), channel_id=1, source_target_pairs={{0,3},{1,2},{2,1},{3,0},{4,7},{5,6},{6,5},{7,4},{8,11},{9,10},{10,... | collective-permute-start | bytes 221192 | tf_op jit(solution)/shard_map/ppermute | solution.py:29
  22.5 6.4 %collective-permute-start.4 = (f32[72,256]{1,0:T(8,128)S(1)}, f32[72,256]{1,0:T(8,128)S(1)}, u32[]{:S(2)}, u32[]{:S(2)}) collective-permute-start(f32[72,256]{1,0:T(8,128)S(1)} %get-tuple-element.22), channel_id=1, source_target_pairs={{0,2},{1,3},{2,0},{3,1},{4,6},{5,7},{6,4},{7,5},{8,10},{9,11},{10,... | collective-permute-start | bytes 221192 | tf_op jit(solution)/shard_map/ppermute | solution.py:29
  22.5 6.4 %collective-permute-start.5 = (f32[72,256]{1,0:T(8,128)S(1)}, f32[72,256]{1,0:T(8,128)S(1)}, u32[]{:S(2)}, u32[]{:S(2)}) collective-permute-start(f32[72,256]{1,0:T(8,128)S(1)} %get-tuple-element.23), channel_id=1, source_target_pairs={{0,1},{1,0},{2,3},{3,2},{4,5},{5,4},{6,7},{7,6},{8,9},{9,8},{10,11... | collective-permute-start | bytes 221192 | tf_op jit(solution)/shard_map/ppermute | solution.py:29

commit v3 on v2

--- a/solution.py
+++ b/solution.py
@@ -14,7 +14,7 @@
 HALF = LANES // 2
 STEP_USERS = 4
 AHEAD = 2
-SPLIT = False
+SPLIT = True
 
 
 def partner_of(rank, offset, size):
@@ -173,7 +173,7 @@
 
     col_head = lax.broadcasted_iota(jnp.int32, (cands, width), 1) // head_size
 
-    def one_user(slot, place, held):
+    def score_user(slot, place, held):
         user = partner_of(rank, offsets[slot], seq_count) * local_users + place
         query = query_buf[user]
         stacked = jnp.concatenate(
@@ -183,11 +183,17 @@
             ],
             axis=0,
         )
-        scores = lax.dot_general(
-            stacked,
-            key_buf[held],
-            (((1,), (1,)), ((), ())),
-            preferred_element_type=jnp.float32,
+        scores = jnp.concatenate(
+            [
+                lax.dot_general(
+                    query[:, head * head_size : (head + 1) * head_size],
+                    key_buf[held, :, head * head_size : (head + 1) * head_size],
+                    (((1,), (1,)), ((), ())),
+                    preferred_element_type=jnp.float32,
+                )
+                for head in range(head_count)
+            ],
+            axis=0,
         )
         biases = jnp.concatenate(
             [
@@ -196,7 +202,9 @@
             ],
             axis=0,
         )
-        scores = scores * scale + biases
+        return scores * scale + biases
+
+    def weigh_user(slot, place, held, scores):
         block_max = jnp.max(scores, axis=1, keepdims=True)
         weights = jnp.exp(scores - block_max)
         block_sum = jnp.sum(weights, axis=1, keepdims=True)
@@ -213,14 +221,24 @@
             block_max, 0
         ) + column_to_row(block_sum, HALF)
 
+    pending = []
     for number, (slot, place) in enumerate(steps):
-        for copy in copies(number):
-            copy.wait()
+        copies(number)[0].wait()
+        if number:
+            copies(number - 1)[1].wait()
         if number + ahead < len(steps):
             for copy in copies(number + ahead):
                 copy.start()
+        scored = []
         for member in range(step_users):
-            one_user(slot, place + member, number * step_users + member)
+            task = (slot, place + member, number * step_users + member)
+            scored.append(task + (score_user(*task),))
+        for task in pending:
+            weigh_user(*task)
+        pending = scored
+    copies(len(steps) - 1)[1].wait()
+    for task in pending:
+        weigh_user(*task)
 
     if not with_own:
         return
@@ -393,7 +411,7 @@
         )(*[pltpu.with_memory_space_constraint(operand, pltpu.HBM) for operand in operands])
 
     order = list(reversed(range(seq_count)))
-    cut = len(order) // 2 if SPLIT else 0
+    cut = len(order) - 1 if SPLIT else 0
     received = []
     for offsets, with_own in ((order[:cut], False), (order[cut:], True)):
         if not offsets:

time: 29.8 us -> 25.6 us (0.86)
  waiting for transfers between devices: 9.86 us -> 6.49 us
  Pallas kernels: 12 us -> 11.2 us
    ppermute x6, waiting for transfers between devices: 9.86 us -> 6.49 us  [exchange(): return lax.ppermute(packet, axis, pairs)]
    pallas_call x1 -> x2, Pallas kernels: 10.6 us -> 9.81 us  [attend(): pl.pallas_call(functools.partial(attend_kernel, offsets=offsets, seq_coun...]
  transfers between devices with their start and end apart: 6 -> 6, of which waited for: 4 -> 3; matrix products, arithmetic and copies ran while one was open for 0% -> 0% of each run, Pallas kernels for 0% -> 13%
where the time goes in v3:
time: 25.6 us; the launch traced here: 25.5 us
  Pallas kernels  11.2 us (44%)
  starting transfers between devices  7.74 us (30%)
  waiting for transfers between devices  6.49 us (25%)
    pallas_call x2, Pallas kernels, attend(): pl.pallas_call(functools.partial(attend_kernel, offsets=offsets, seq_coun...  9.81 us
    ppermute x6, starting transfers between devices, exchange(): return lax.ppermute(packet, axis, pairs)  7.74 us
    ppermute x6, waiting for transfers between devices, exchange(): return lax.ppermute(packet, axis, pairs)  6.49 us
    pallas_call x1, Pallas kernels, body(): pl.pallas_call(functools.partial(finish_kernel, full_width=width * head_a...  0.73 us
    pallas_call x1, Pallas kernels, body(): pl.pallas_call(functools.partial(project_kernel, cands=cands, source_coun...  0.64 us
  transfers between devices with their start and end apart: 6, of which 3 were waited for; matrix products, arithmetic and copies ran while one was open for 0% of the time, Pallas kernels for 13%

profile of v3, /device:TPU:0, one launch (start us, length us, event | category | flops | bytes accessed | tf_op | source)
XLA Modules:
  0.0 25.5 jit_solution(4872960857978653834)
XLA Ops:
  0.0 6.5 %attend.2 = (f32[136,128]{1,0:T(8,128)S(1)}, f32[136,128]{1,0:T(8,128)S(1)}, f32[136,128]{1,0:T(8,128)S(1)}) custom-call(bf16[16,16,256]{2,1,0:T(8,128)(2,1)} %refs_0_.3, bf16[16,1024,256]{2,1,0:T(8,128)(2,1)} %refs_1_.3, bf16[16,1024,256]{2,1,0:T(8,128)(2,1)} %refs_2_.3, s32[16]{0:T(128)} %refs_3_.3, s32[16,1024]{1,0:T(8,128)} %refs_4_.3, ...), custom_call_target="tpu_custom_call" | custom-call | tf_op jit(solution)/shard_map/attend/pallas_call | solution.py:396
  6.5 2.5 %collective-permute-start = (f32[136,128]{1,0:T(8,128)S(1)}, f32[136,128]{1,0:T(8,128)S(1)}, u32[]{:S(2)}, u32[]{:S(2)}) collective-permute-start(f32[136,128]{1,0:T(8,128)S(1)} %get-tuple-element.15), channel_id=1, source_target_pairs={{0,12},{4,8},{8,4},{12,0},{1,13},{5,9},{9,5},{13,1},{2,14},{6,10},... | collective-permute-start | bytes 208904 | tf_op jit(solution)/shard_map/ppermute | solution.py:29
  9.0 0.6 %collective-permute-start.1 = (f32[136,128]{1,0:T(8,128)S(1)}, f32[136,128]{1,0:T(8,128)S(1)}, u32[]{:S(2)}, u32[]{:S(2)}) collective-permute-start(f32[136,128]{1,0:T(8,128)S(1)} %get-tuple-element.16), channel_id=1, source_target_pairs={{0,8},{4,12},{8,0},{12,4},{1,9},{5,13},{9,1},{13,5},{2,10},{6,14},... | collective-permute-start | bytes 208904 | tf_op jit(solution)/shard_map/ppermute | solution.py:29
  9.6 0.0 copy-start
  9.6 0.0 collective-permute-start.2
  9.7 3.4 %attend.3 = (f32[136,128]{1,0:T(8,128)S(1)}, f32[136,128]{1,0:T(8,128)S(1)}, f32[64,256]{1,0:T(8,128)S(1)}) custom-call(bf16[16,16,256]{2,1,0:T(8,128)(2,1)} %refs_0_.3, bf16[16,1024,256]{2,1,0:T(8,128)(2,1)} %refs_1_.3, bf16[16,1024,256]{2,1,0:T(8,128)(2,1)} %refs_2_.3, s32[16]{0:T(128)} %refs_3_.3, s32[16,1024]{1,0:T(8,128)} %refs_4_.3, ...), custom_call_target="tpu_custom_call" | custom-call | tf_op jit(solution)/shard_map/attend/pallas_call | solution.py:396
  13.0 0.0 collective-permute-done.refs_0_
  13.0 0.7 %collective-permute-done.1.refs_1_ = f32[136,128]{1,0:T(8,128)S(1)} collective-permute-done((f32[136,128]{1,0:T(8,128)S(1)}, f32[136,128]{1,0:T(8,128)S(1)}, u32[]{:S(2)}, u32[]{:S(2)}) %collective-permute-start.1) | collective-permute-done | bytes 69664 | tf_op jit(solution)/shard_map/ppermute | solution.py:29
  13.7 0.0 collective-permute-done.2.refs_2_
  13.7 0.0 copy-done
  13.7 0.6 %project.1 = (f32[72,256]{1,0:T(8,128)S(1)}, f32[72,256]{1,0:T(8,128)S(1)}, f32[72,256]{1,0:T(8,128)S(1)}, f32[72,256]{1,0:T(8,128)S(1)}) custom-call(f32[136,128]{1,0:T(8,128)S(1)} %collective-permute-done.refs_0_, f32[136,128]{1,0:T(8,128)S(1)} %collective-permute-done.1.refs_1_, f32[136,128]{1,0:T(8,128)S(1)} %collective-permute-done.2.refs_2_, ...), custom_call_target="tpu_custom_call" | custom-call | tf_op jit(solution)/shard_map/project/pallas_call | solution.py:425
  14.4 3.9 %collective-permute-start.3 = (f32[72,256]{1,0:T(8,128)S(1)}, f32[72,256]{1,0:T(8,128)S(1)}, u32[]{:S(2)}, u32[]{:S(2)}) collective-permute-start(f32[72,256]{1,0:T(8,128)S(1)} %get-tuple-element.21), channel_id=1, source_target_pairs={{0,3},{1,2},{2,1},{3,0},{4,7},{5,6},{6,5},{7,4},{8,11},{9,10},{10,... | collective-permute-start | bytes 221192 | tf_op jit(solution)/shard_map/ppermute | solution.py:29
  18.3 0.0 collective-permute-start.4
  18.3 0.6 %collective-permute-start.5 = (f32[72,256]{1,0:T(8,128)S(1)}, f32[72,256]{1,0:T(8,128)S(1)}, u32[]{:S(2)}, u32[]{:S(2)}) collective-permute-start(f32[72,256]{1,0:T(8,128)S(1)} %get-tuple-element.23), channel_id=1, source_target_pairs={{0,1},{1,0},{2,3},{3,2},{4,5},{5,4},{6,7},{7,6},{8,9},{9,8},{10,11... | collective-permute-start | bytes 221192 | tf_op jit(solution)/shard_map/ppermute | solution.py:29
  18.9 2.2 %collective-permute-done.3.refs_0_ = f32[72,256]{1,0:T(8,128)S(1)} collective-permute-done((f32[72,256]{1,0:T(8,128)S(1)}, f32[72,256]{1,0:T(8,128)S(1)}, u32[]{:S(2)}, u32[]{:S(2)}) %collective-permute-start.3) | collective-permute-done | bytes 73760 | tf_op jit(solution)/shard_map/ppermute | solution.py:29
  21.1 3.6 %collective-permute-done.4.refs_1_ = f32[72,256]{1,0:T(8,128)S(1)} collective-permute-done((f32[72,256]{1,0:T(8,128)S(1)}, f32[72,256]{1,0:T(8,128)S(1)}, u32[]{:S(2)}, u32[]{:S(2)}) %collective-permute-start.4) | collective-permute-done | bytes 73760 | tf_op jit(solution)/shard_map/ppermute | solution.py:29
  24.7 0.0 collective-permute-done.5.refs_2_
  24.7 0.7 %finish.1 = bf16[4,16,256]{2,1,0:T(8,128)(2,1)} custom-call(f32[72,256]{1,0:T(8,128)S(1)} %collective-permute-done.3.refs_0_, f32[72,256]{1,0:T(8,128)S(1)} %collective-permute-done.4.refs_1_, f32[72,256]{1,0:T(8,128)S(1)} %collective-permute-done.5.refs_2_, f32[72,256]{1,0:T(8,128)S(1)} %get-tuple-element.24.refs_3_), custom_call_target="tpu_custom_call" | custom-call | tf_op jit(solution)/shard_map/finish/pallas_call | solution.py:441
Async XLA Ops:
  6.5 6.5 %collective-permute-start = (f32[136,128]{1,0:T(8,128)S(1)}, f32[136,128]{1,0:T(8,128)S(1)}, u32[]{:S(2)}, u32[]{:S(2)}) collective-permute-start(f32[136,128]{1,0:T(8,128)S(1)} %get-tuple-element.15), channel_id=1, source_target_pairs={{0,12},{4,8},{8,4},{12,0},{1,13},{5,9},{9,5},{13,1},{2,14},{6,10},... | collective-permute-start | bytes 208904 | tf_op jit(solution)/shard_map/ppermute | solution.py:29
  9.0 4.8 %collective-permute-start.1 = (f32[136,128]{1,0:T(8,128)S(1)}, f32[136,128]{1,0:T(8,128)S(1)}, u32[]{:S(2)}, u32[]{:S(2)}) collective-permute-start(f32[136,128]{1,0:T(8,128)S(1)} %get-tuple-element.16), channel_id=1, source_target_pairs={{0,8},{4,12},{8,0},{12,4},{1,9},{5,13},{9,1},{13,5},{2,10},{6,14},... | collective-permute-start | bytes 208904 | tf_op jit(solution)/shard_map/ppermute | solution.py:29
  9.6 4.1 %copy-start = (bf16[256,1024]{1,0:T(8,128)(2,1)S(1)}, bf16[256,1024]{1,0:T(8,128)(2,1)}, u32[]{:S(2)}) copy-start(bf16[256,1024]{1,0:T(8,128)(2,1)} %refs_6_.1) | copy-start | bytes 1572868
  9.6 4.1 %collective-permute-start.2 = (f32[136,128]{1,0:T(8,128)S(1)}, f32[136,128]{1,0:T(8,128)S(1)}, u32[]{:S(2)}, u32[]{:S(2)}) collective-permute-start(f32[136,128]{1,0:T(8,128)S(1)} %get-tuple-element.17), channel_id=1, source_target_pairs={{0,4},{4,0},{8,12},{12,8},{1,5},{5,1},{9,13},{13,9},{2,6},{6,2},{1... | collective-permute-start | bytes 208904 | tf_op jit(solution)/shard_map/ppermute | solution.py:29
  14.4 6.7 %collective-permute-start.3 = (f32[72,256]{1,0:T(8,128)S(1)}, f32[72,256]{1,0:T(8,128)S(1)}, u32[]{:S(2)}, u32[]{:S(2)}) collective-permute-start(f32[72,256]{1,0:T(8,128)S(1)} %get-tuple-element.21), channel_id=1, source_target_pairs={{0,3},{1,2},{2,1},{3,0},{4,7},{5,6},{6,5},{7,4},{8,11},{9,10},{10,... | collective-permute-start | bytes 221192 | tf_op jit(solution)/shard_map/ppermute | solution.py:29
  18.3 6.4 %collective-permute-start.4 = (f32[72,256]{1,0:T(8,128)S(1)}, f32[72,256]{1,0:T(8,128)S(1)}, u32[]{:S(2)}, u32[]{:S(2)}) collective-permute-start(f32[72,256]{1,0:T(8,128)S(1)} %get-tuple-element.22), channel_id=1, source_target_pairs={{0,2},{1,3},{2,0},{3,1},{4,6},{5,7},{6,4},{7,5},{8,10},{9,11},{10,... | collective-permute-start | bytes 221192 | tf_op jit(solution)/shard_map/ppermute | solution.py:29
  18.3 6.4 %collective-permute-start.5 = (f32[72,256]{1,0:T(8,128)S(1)}, f32[72,256]{1,0:T(8,128)S(1)}, u32[]{:S(2)}, u32[]{:S(2)}) collective-permute-start(f32[72,256]{1,0:T(8,128)S(1)} %get-tuple-element.23), channel_id=1, source_target_pairs={{0,1},{1,0},{2,3},{3,2},{4,5},{5,4},{6,7},{7,6},{8,9},{9,8},{10,11... | collective-permute-start | bytes 221192 | tf_op jit(solution)/shard_map/ppermute | solution.py:29
